TPU v7x, 32 devices: a whole 2x2x4 slice. The times are simulated.
32 devices in a mesh: seq: 8 (over z, y), head: 4 (over x, core).
Axes of the slice: x: 2, y: 2, z: 4, core: 2. Of those that a mesh axis runs over, the one named last changes fastest.
Arguments:
- layer_in: bfloat16 [4096, 2048], P('seq', 'head'), may hold values from -6 to 6
- query_weight: bfloat16 [2048, 1024], P(None, 'head'), may hold values from -0.125 to 0.125
- key_weight: bfloat16 [2048, 1024], P(None, 'head'), may hold values from -0.125 to 0.125
- value_weight: bfloat16 [2048, 1024], P(None, 'head'), may hold values from -0.125 to 0.125
- gate_weight: bfloat16 [2048, 1024], P(None, 'head'), may hold values from -0.125 to 0.125
- beta_weight: bfloat16 [2048, 8], P(None, 'head'), may hold values from -0.125 to 0.125
- decay_weight: bfloat16 [2048, 8], P(None, 'head'), may hold values from -0.125 to 0.125
- conv_weight: float32 [4, 3, 1024], P(None, None, 'head'), may hold values from -3 to 3
- decay_log: float32 [8], P('head'), as said below
- beta_bias: float32 [8], P('head'), as said below
- decay_bias: float32 [8], P('head'), may hold values from -1 to 1
- norm_gain: float32 [128], replicated, may hold values from 0.1 to 1.9
- out_weight: bfloat16 [1024, 2048], P('head'), may hold values from -0.1875 to 0.1875
Outputs:
- layer_out: bfloat16 [4096, 2048], P('seq', 'head')
Inputs may be any that keep to these rules, and one draw needn't show every extreme that they name: decay_log lies between log(0.1 / 4096) and log(0.05). beta_bias lies between log(0.5 * 128 / 4096) and 1.
All inputs are finite; a program needn't handle non-finite values.
Results may differ from a plain program's by a relative error of at most 0.0049.
Values may be sent and summed in bfloat16 or wider, within the bound.
A program may use at most 128 MiB of HBM per device.

v0:
```python
import jax
import jax.numpy as jnp
from jax import lax
from jax.sharding import PartitionSpec as P

BLOCK = 128


exact_mode = lax.Precision.HIGHEST
norm_floor = 0.0001


def passed_along(value, axis, steps):
    count = lax.axis_size(axis)
    leading, last = (max(0, -steps), min(count, count - steps))
    return lax.ppermute(value, axis, [(source, source + steps) for source in range(leading, last)])


def causal_conv(values, earlier, kernel):
    reach_back = kernel.shape[0] - 1
    tokens = values.shape[0]
    extended = jnp.concatenate([earlier, values], axis=0)
    summed = kernel[0] * values
    for offset in range(1, reach_back + 1):
        summed = (
            summed + kernel[offset] * extended[reach_back - offset : reach_back - offset + tokens]
        )
    return jax.nn.silu(summed)


def unit_rows(values):
    return values * lax.rsqrt(jnp.sum(values * values, axis=-1, keepdims=True) + 1.0)


def unit_lower_inverse(system):
    length = system.shape[-1]
    row_index = lax.broadcasted_iota(jnp.int32, (length, length), 0)
    col_index = lax.broadcasted_iota(jnp.int32, (length, length), 1)
    inverse = jnp.broadcast_to(jnp.eye(length, dtype=jnp.float32), system.shape)
    width = 1
    while width < length:
        same_pair = row_index // (2 * width) == col_index // (2 * width)
        lower_half = row_index // width > col_index // width
        linking = jnp.where(same_pair & lower_half, system, 0.0)
        middle = lax.optimization_barrier(
            jnp.einsum("...rs,...st->...rt", linking, inverse, precision=exact_mode)
        )
        update = lax.optimization_barrier(
            jnp.einsum("...rs,...st->...rt", inverse, middle, precision=exact_mode)
        )
        inverse = inverse - update
        width = width * 2
    return inverse


def block_terms(queries, key_rows, values, beta_gate, log_decay):
    length = log_decay.shape[-1]
    running = jnp.cumsum(log_decay, axis=-1)
    row_index = lax.broadcasted_iota(jnp.int32, (length, length), 0)
    col_index = lax.broadcasted_iota(jnp.int32, (length, length), 1)
    within = row_index >= col_index
    before = row_index > col_index
    spread = running[..., :, None] - running[..., None, :]
    decay_matrix = jnp.where(within, jnp.exp(jnp.minimum(spread, 0.0)), 0.0)
    key_gram = jnp.einsum("...rd,...sd->...rs", key_rows, key_rows, precision=exact_mode)
    lower_part = jnp.where(before, beta_gate[..., :, None] * decay_matrix * key_gram, 0.0)
    system = lower_part + jnp.eye(length, dtype=jnp.float32)
    growth = jnp.exp(running)
    right_side = jnp.concatenate(
        [beta_gate[..., None] * values, (beta_gate * growth)[..., None] * key_rows], axis=-1
    )
    solved = jnp.einsum(
        "...rs,...se->...re", unit_lower_inverse(system), right_side, precision=exact_mode
    )
    value_dim = values.shape[-1]
    fixed_rows = solved[..., :value_dim]
    erased = solved[..., value_dim:]
    query_key = jnp.einsum("...rd,...sd->...rs", queries, key_rows, precision=exact_mode)
    mixing = jnp.where(within, decay_matrix * query_key, 0.0)
    local_out = jnp.einsum("...rs,...se->...re", mixing, fixed_rows, precision=exact_mode)
    removed = lax.optimization_barrier(
        jnp.einsum("...rs,...sd->...rd", mixing, erased, precision=exact_mode)
    )
    reader = growth[..., None] * queries - removed
    tail_decay = jnp.exp(running[..., -1:] - running)
    weighted = tail_decay[..., None] * key_rows
    key_dim = key_rows.shape[-1]
    lost_part = lax.optimization_barrier(
        jnp.einsum("...bd,...be->...de", weighted, erased, precision=exact_mode)
    )
    transit = (
        jnp.exp(running[..., -1])[..., None, None] * jnp.eye(key_dim, dtype=jnp.float32) - lost_part
    )
    carried = jnp.einsum("...bd,...be->...de", weighted, fixed_rows, precision=exact_mode)
    return (local_out, reader, transit, carried)


def compose(earlier, later_map):
    joined = jnp.einsum("...de,...ef->...df", later_map[0], earlier[0], precision=exact_mode)
    moved = (
        jnp.einsum("...de,...ef->...df", later_map[0], earlier[1], precision=exact_mode)
        + later_map[1]
    )
    return (joined, moved)


def on_device(
    layer_in,
    query_weight,
    key_weight,
    value_weight,
    gate_weight,
    beta_weight,
    decay_weight,
    conv_weight,
    decay_log,
    beta_bias,
    decay_bias,
    norm_gain,
    out_weight,
):
    tokens = layer_in.shape[0]
    head_count = beta_weight.shape[1]
    head_dim = query_weight.shape[1] // head_count
    weights = (query_weight, key_weight, value_weight, gate_weight, beta_weight, decay_weight)
    shard_piece = lax.all_gather(layer_in, "head", axis=1, tiled=True)
    query_raw, key_raw, value_raw, gate_raw, beta_raw, decay_raw = tuple(
        (jnp.dot(shard_piece, weight, preferred_element_type=jnp.float32) for weight in weights)
    )
    reach_back = conv_weight.shape[0] - 1
    channels = query_raw.shape[1]
    last_rows = jnp.concatenate(
        [
            query_raw[tokens - reach_back :],
            key_raw[tokens - reach_back :],
            value_raw[tokens - reach_back :],
        ],
        axis=1,
    )
    prior_rows = passed_along(last_rows, "seq", 1)
    mixed_query = causal_conv(query_raw, prior_rows[:, :channels], conv_weight[:, 0])
    mixed_key = causal_conv(key_raw, prior_rows[:, channels : 2 * channels], conv_weight[:, 1])
    mixed_value = causal_conv(value_raw, prior_rows[:, 2 * channels :], conv_weight[:, 2])
    queries = unit_rows(mixed_query.reshape(tokens, head_count, head_dim))
    key_rows = unit_rows(mixed_key.reshape(tokens, head_count, head_dim))
    values = mixed_value.reshape(tokens, head_count, head_dim)
    beta_gate = jax.nn.sigmoid(beta_raw + beta_bias)
    log_decay = -jnp.exp(decay_log) * jax.nn.softplus(decay_raw + decay_bias)
    blocks = tokens // BLOCK

    def arrange(array):
        return array.reshape(blocks, BLOCK, head_count, head_dim).transpose(0, 2, 1, 3)

    def arrange_gate(array):
        return array.reshape(blocks, BLOCK, head_count).transpose(0, 2, 1)

    local_out, reader, transit, carried = block_terms(
        arrange(queries),
        arrange(key_rows),
        arrange(values),
        arrange_gate(beta_gate),
        arrange_gate(log_decay),
    )
    identity = jnp.broadcast_to(
        jnp.eye(head_dim, dtype=jnp.float32), (head_count, head_dim, head_dim)
    )
    nothing = jnp.zeros((head_count, head_dim, head_dim), jnp.float32)

    def through(running_pair, block_maps):
        return (compose(running_pair, block_maps), None)

    slab_pair, unused_rest = lax.scan(through, (identity, nothing), (transit, carried))
    slab_transit, slab_state = slab_pair
    stacked = jnp.stack([slab_transit, slab_state], axis=0)[None]
    every_map = lax.all_gather(stacked, "seq", axis=0, tiled=True)
    every_transit = every_map[:, 0]
    every_state = every_map[:, 1]
    position = lax.axis_index("seq")
    order = lax.broadcasted_iota(jnp.int32, (every_transit.shape[0], 1, 1, 1), 0)
    earlier_ones = order < position
    affine = (
        jnp.where(earlier_ones, every_transit, identity[None]),
        jnp.where(earlier_ones, every_state, 0.0),
    )
    while affine[0].shape[0] > 1:
        affine = compose((affine[0][0::2], affine[1][0::2]), (affine[0][1::2], affine[1][1::2]))
    incoming = affine[1][0]

    def advance(carry_state, block_maps):
        following = (
            jnp.einsum("hde,hef->hdf", block_maps[0], carry_state, precision=exact_mode)
            + block_maps[1]
        )
        return (following, carry_state)

    unused_last, starts = lax.scan(advance, incoming, (transit, carried))
    outputs = local_out + jnp.einsum("nhrd,nhde->nhre", reader, starts, precision=exact_mode)
    head_out = outputs.transpose(0, 2, 1, 3).reshape(tokens, head_count, head_dim)
    gate_rows = gate_raw.reshape(tokens, head_count, head_dim)
    scaled = head_out * lax.rsqrt(
        jnp.mean(head_out * head_out, axis=-1, keepdims=True) + norm_floor
    )
    hidden = (
        (scaled * norm_gain * jax.nn.silu(gate_rows))
        .reshape(tokens, head_count * head_dim)
        .astype(jnp.bfloat16)
    )
    column_weight = lax.all_to_all(out_weight, "head", split_axis=1, concat_axis=0, tiled=True)
    summed = jnp.dot(
        lax.all_gather(hidden, "head", axis=1, tiled=True),
        column_weight,
        preferred_element_type=jnp.float32,
    )
    return summed.astype(jnp.bfloat16)


def solution(mesh):
    return jax.shard_map(
        on_device,
        mesh=mesh,
        in_specs=(
            P("seq", "head"),
            P(None, "head"),
            P(None, "head"),
            P(None, "head"),
            P(None, "head"),
            P(None, "head"),
            P(None, "head"),
            P(None, None, "head"),
            P("head"),
            P("head"),
            P("head"),
            P(),
            P("head", None),
        ),
        out_specs=P("seq", "head"),
        check_vma=False,
    )
```

profile of v0, /device:TPU:0, one launch (start us, length us, event | category | flops | bytes accessed | tf_op | source)
XLA Modules:
  0.0 182.9 jit_solution(447879425216133817)
XLA Ops:
  6.5 0.7 all-gather.5.cloned.1.call-update
  7.5 1.2 exponential_negate_fusion
  8.7 1.5 fusion.147
  10.7 23.5 %all-gather.5.cloned.1.call-done = bf16[512,2048]{1,0:T(8,128)(2,1)} async-done(((bf16[512,512]{1,0:T(8,128)(2,1)}), bf16[512,2048]{1,0:T(8,128)(2,1)}) %all-gather.5.cloned.1.call-update) | async-done | bytes 2097168 | tf_op jit(solution)/shard_map/all_gather | solution.py:126
  34.2 2.4 %fusion.135 = f32[4,2,128]{2,1,0:T(2,128)S(1)} fusion(bf16[512,2048]{1,0:T(8,128)(2,1)} %all-gather.5.cloned.1.call-done, bf16[2048,2]{0,1:T(2,128)(2,1)} %param.23, f32[2]{0:T(128)} %param.27, f32[2]{0:T(128)} %exponential_negate_fusion), kind=kOutput, calls=%fused_computation.194 | convolution fusion | flops 4202496 | bytes 2109456 | tf_op jit(solution)/shard_map/dot_general | solution.py:128
  36.7 1.2 reduce_window_sum.11
  38.2 0.7 fusion.152
  39.4 0.7 fusion.151
  40.1 0.8 copy-done.7
  40.9 0.7 fusion.150
  41.7 3.6 %collective-permute-start = (f32[3,768]{1,0:T(4,128)S(1)}, f32[3,768]{1,0:T(4,128)S(1)}, u32[]{:S(2)}, u32[]{:S(2)}) collective-permute-start(f32[3,768]{1,0:T(4,128)S(1)} %pad_maximum_fusion.4), channel_id=1, source_target_pairs={{0,4},{4,8},{8,12},{12,16},{16,20},{20,24},{24,28},{1,5},{5,9},{9,... | collective-permute-start | bytes 27656 | tf_op jit(solution)/shard_map/ppermute | solution.py:16
  45.3 0.7 fusion.149
  46.5 2.2 %fusion.146 = (f32[512,256]{1,0:T(8,128)S(1)}, f32[512,256]{1,0:T(8,128)S(1)}) fusion(f32[512,256]{1,0:T(8,128)} %copy-done.7, f32[3,256]{1,0:T(4,128)S(1)} %get-tuple-element.120, f32[256]{0:T(256)} %bitcast.193, f32[256]{0:T(256)} %bitcast.194, f32[256]{0:T(256)} %bitcast.195, f32[256]{0:T(256)} %bitcast.196), kind=kLoop, calls=%fused_computation.241 | loop fusion | flops 1966080 | bytes 1580032 | tf_op jit(solution)/shard_map/mul | solution.py:32
  50.0 1.4 fusion.16
  52.6 0.7 fusion.77
  53.3 0.7 fusion.91
  54.0 0.7 fusion.75
  54.7 0.6 fusion.153
  55.4 0.7 fusion.73
  56.1 0.6 fusion.154
  56.8 0.7 fusion.71
  57.5 0.6 fusion.155
  58.2 0.7 fusion.69
  58.8 0.6 fusion.156
  59.6 0.9 fusion.67
  60.5 1.4 fusion.157
  62.0 1.1 bitcast_multiply_fusion.3
  63.2 1.6 fusion.145
  65.3 2.2 %fusion.27 = f32[4,2,128,256]{3,2,1,0:T(8,128)S(1)} fusion(f32[4,2,128,128]{3,2,1,0:T(8,128)} %bitcast_multiply_fusion.3, f32[4,2,128,128]{3,2,1,0:T(8,128)S(1)} %bitcast_multiply_fusion.1, f32[4,2,128,128]{3,2,1,0:T(8,128)S(1)} %sub.166, f32[4,2,128,128]{3,2,1,0:T(8,128)} %fusion.157), kind=kOutput, calls=%fused_computation.42 | convolution fusion | flops 403046400 | bytes 3145728 | tf_op jit(solution)/shard_map/...rs,...se->...re/dot_general | solution.py:72
  67.5 2.1 %fusion.81 = f32[4,2,128,128]{3,2,1,0:T(8,128)} fusion(f32[4,2,128,256]{3,2,1,0:T(8,128)S(1)} %fusion.27, f32[4,128,2,128]{3,2,1,0:T(2,128)S(1)} %reshape.141, f32[4,2,128]{2,1,0:T(2,128)S(1)} %get-tuple-element.124, f32[4,128,2]{1,2,0:T(2,128)S(1)} %bitcast.179), kind=kOutput, calls=%fused_computation.117 | convolution fusion | flops 201588736 | bytes 1581056 | tf_op jit(solution)/shard_map/...bd,...be->...de/dot_general | solution.py:94
  69.6 1.3 fusion.82
  71.0 6.0 %while.28 = (s32[]{:T(128)}, f32[2,128,128]{2,1,0:T(8,128)S(1)}, f32[2,128,128]{2,1,0:T(8,128)S(1)}, f32[4,2,128,128]{3,2,1,0:T(8,128)S(1)}, f32[4,2,128,128]{3,2,1,0:T(8,128)}) while((s32[]{:T(128)}, f32[2,128,128]{2,1,0:T(8,128)S(1)}, f32[2,128,128]{2,1,0:T(8,128)S(1)}, f32[4,2,128,128]{3,2,1,0:T(8,128)S(1)}, ...), condition=%wide.region_4.5_spmd.clone.clone, body=%wide.region_3.4_spmd.clone.sunk.clone | while | flops 100728832 | bytes 1443410 | solution.py:172
  71.1 1.2 convolution_add_fusion.12
  72.6 1.2 convolution_add_fusion.12
  74.1 1.2 convolution_add_fusion.12
  75.6 1.2 convolution_add_fusion.12
  77.1 0.7 pad_maximum_fusion.3
  77.9 2.1 %mul.279 = f32[512,2,128]{2,1,0:T(2,128)} reshape(f32[512,256]{1,0:T(8,128)} %get-tuple-element.101) | data formatting | bytes 1048576 | tf_op jit(solution)/shard_map/mul | solution.py:32
  80.0 2.4 %reduce_sum.27 = f32[512,2]{1,0:T(8,128)} reduce(f32[512,2,128]{2,1,0:T(2,128)} %mul.279, f32[]{:T(128)} %constant.223.clone.1), dimensions={2}, to_apply=%region_1.2 | reduce | flops 130048 | bytes 528388 | tf_op jit(solution)/shard_map/reduce_sum | solution.py:32
  82.4 1.7 add_rsqrt_fusion.1
  84.1 1.1 copy.116
  85.2 2.1 %reshape.140 = f32[4,128,2,128]{3,2,1,0:T(2,128)} reshape(f32[512,256]{1,0:T(8,128)} %get-tuple-element.102) | data formatting | bytes 1048576 | tf_op jit(solution)/shard_map/reshape | solution.py:144
  87.3 2.4 %fusion.17 = f32[4,2,128,128]{3,2,1,0:T(8,128)S(1)} fusion(f32[4,128,2,128]{3,2,1,0:T(2,128)} %reshape.140, f32[4,128,2,128]{3,2,1,0:T(2,128)S(1)} %reshape.141, f32[4,128,2]{1,2,0:T(2,128)S(1)} %bitcast.181, f32[4,128,2]{1,2,0:T(2,128)S(1)} %bitcast.182, f32[4,2,128]{2,1,0:T(2,128)S(1)} %reduce_window_sum.11, pred[128,128]{1,0:T(8,128)(4,1)S(1)} %get-tuple-element.137), kind=kOutput, calls=%fused_computation.25 | convolution fusion | flops 202244096 | bytes 1601536 | tf_op jit(solution)/shard_map/...rd,...sd->...rs/dot_general | solution.py:78
  89.7 1.5 fusion.84
  91.2 1.8 fusion.87
  92.9 35.0 %all-gather.9.cloned.1.call-done = f32[16,2,128,128]{3,2,1,0:T(8,128)} async-done(((f32[2,2,128,128]{3,2,1,0:T(8,128)}), f32[16,2,128,128]{3,2,1,0:T(8,128)}) %all-gather.9.cloned.1.call-update) | async-done | bytes 2097168 | tf_op jit(solution)/shard_map/all_gather | solution.py:175
  127.9 1.8 %fusion.25 = (f32[8,2,128,128]{3,2,1,0:T(8,128)S(1)}, f32[8,2,128,128]{3,2,1,0:T(8,128)S(1)}) fusion(f32[8,2,2,128,128]{4,3,2,1,0:T(8,128)} %bitcast.173, pred[8]{0:T(512)(128)(4,1)S(1)} %iota_compare_fusion.3, f32[128,128]{1,0:T(8,128)S(1)} %fusion.133), kind=kLoop, calls=%fused_computation.39 | loop fusion | flops 524288 | bytes 4259848 | tf_op jit(solution)/shard_map/jit(_where)/select_n | solution.py:183
  129.7 0.7 fusion.64
  130.4 0.7 convolution_add_fusion.3
  132.0 7.5 %while.27 = (s32[]{:T(128)}, f32[2,128,128]{2,1,0:T(8,128)S(1)}, f32[4,2,128,128]{3,2,1,0:T(8,128)}, f32[4,2,128,128]{3,2,1,0:T(8,128)S(1)}, f32[4,2,128,128]{3,2,1,0:T(8,128)}) while((s32[]{:T(128)}, f32[2,128,128]{2,1,0:T(8,128)S(1)}, f32[4,2,128,128]{3,2,1,0:T(8,128)}, f32[4,2,128,128]{3,2,1,0:T(8,128)S(1)}, ...), condition=%wide.region_6.7_spmd.clone, body=%wide.region_5.6_spmd.sunk.clone | while | flops 50364416 | bytes 1049673 | solution.py:196
  132.1 0.7 bitcast_dynamic-update-slice_fusion.3
  132.7 1.2 convolution_add_fusion.11
  134.0 0.7 bitcast_dynamic-update-slice_fusion.3
  134.6 1.2 convolution_add_fusion.11
  135.8 0.7 bitcast_dynamic-update-slice_fusion.3
  136.5 1.2 convolution_add_fusion.11
  137.7 0.7 bitcast_dynamic-update-slice_fusion.3
  138.4 1.2 convolution_add_fusion.11
  139.6 3.8 %multiply_reduce_fusion = (f32[4,128,2]{1,2,0:T(2,128)S(1)}, f32[4,128,2,128]{1,3,2,0:T(8,128)}) fusion(f32[4,2,128,128]{2,3,1,0:T(8,128)} %fusion.87, f32[4,2,128,128]{3,2,1,0:T(8,128)} %get-tuple-element.62, f32[4,2,128,128]{3,2,1,0:T(8,128)} %fusion.84, f32[4,128,2,128]{3,2,1,0:T(2,128)} %reshape.140, f32[4,2,128]{2,1,0:T(2,128)S(1)} %get-tuple-element.122, ...), kind=kOutput, calls=%fused_computation.93 | convolution fusion | flops 202112000 | bytes 2633728 | tf_op jit(solution)/shard_map/nhrd,nhde->nhre/dot_general | solution.py:197
  143.5 2.0 %copy.104 = f32[4,128,2,128]{3,2,1,0:T(2,128)} copy(f32[4,128,2,128]{1,3,2,0:T(8,128)} %get-tuple-element.134) | data formatting | bytes 1048576 | tf_op jit(solution)/shard_map/add | solution.py:197
  146.2 2.8 %fusion.54 = bf16[512,256]{1,0:T(8,128)(2,1)} fusion(f32[64,8,2,128]{3,2,1,0:T(2,128)S(1)} %bitcast.175, f32[64,8,2,128]{3,2,1,0:T(2,128)} %bitcast.176, f32[256]{0:T(256)S(1)} %broadcast_bitcast_fusion, bf16[512,2048]{1,0:T(8,128)(2,1)S(1)} %copy-done.2, bf16[2048,256]{1,0:T(8,128)(2,1)} %param.21), kind=kOutput, calls=%fused_computation.76 | convolution fusion | flops 537919488 | bytes 4457472 | tf_op jit(solution)/shard_map/dot_general | solution.py:128
  149.0 1.5 copy.106
  150.5 22.6 %all_to_all.19 = bf16[256,4,512]{0,2,1:T(8,128)(2,1)S(1)} all-to-all(bf16[256,4,512]{0,2,1:T(8,128)(2,1)S(1)} %bitcast.172), channel_id=1, replica_groups=mesh['seq'=8,'head'=4] {'head'}, dimensions={1} | all-to-all | bytes 2097152 | tf_op jit(solution)/shard_map/all_to_all | solution.py:208
  173.6 2.7 %convolution_convert_fusion = bf16[512,512]{1,0:T(8,128)(2,1)} fusion(bf16[512,1024]{1,0:T(8,128)(2,1)} %all-gather.7.cloned.1.call-done, bf16[1024,512]{1,0:T(8,128)(2,1)S(1)} %bitcast.174), kind=kOutput, calls=%fused_computation.17 | convolution fusion | flops 537133056 | bytes 2621440 | tf_op jit(solution)/shard_map/dot_general | solution.py:209
  (112 shorter events, 8.9 us)
Async XLA Ops:
  6.5 31.6 %copy-start = (bf16[2048,256]{1,0:T(8,128)(2,1)S(1)}, bf16[2048,256]{1,0:T(8,128)(2,1)}, u32[]{:S(2)}) copy-start(bf16[2048,256]{1,0:T(8,128)(2,1)} %param.20) | copy-start | bytes 3145732
  6.5 27.7 %all-gather.5.cloned.1.call-start = ((), (), s32[]{:S(2)}) async-start(), calls=%async_computation.1 | async-start | bytes 2621440 | tf_op jit(solution)/shard_map/all_gather | solution.py:126
  7.3 120.7 %all-gather.9.cloned.1.call-start = ((), (), s32[]{:S(2)}) async-start(), calls=%async_computation.3 | async-start | bytes 2359296 | tf_op jit(solution)/shard_map/all_gather | solution.py:175
  34.2 3.9 %copy-start.1 = (bf16[512,2048]{1,0:T(8,128)(2,1)S(1)}, bf16[512,2048]{1,0:T(8,128)(2,1)}, u32[]{:S(2)}) copy-start(bf16[512,2048]{1,0:T(8,128)(2,1)} %all-gather.5.cloned.1.call-done) | copy-start | bytes 6291460
  38.2 1.2 copy-start.16
  38.9 2.8 %copy-start.3 = (f32[512,256]{1,0:T(8,128)}, f32[512,256]{1,0:T(8,128)S(1)}, u32[]{:S(2)}) copy-start(f32[512,256]{1,0:T(8,128)S(1)} %fusion.152) | copy-start | bytes 1572868
  38.9 2.0 %copy-start.17 = (bf16[2048,256]{1,0:T(8,128)(2,1)S(1)}, bf16[2048,256]{1,0:T(8,128)(2,1)}, u32[]{:S(2)}) copy-start(bf16[2048,256]{1,0:T(8,128)(2,1)} %param.18) | copy-start | bytes 3145732
  40.1 0.8 copy-start.7
  40.9 4.3 %copy-start.8 = (bf16[2048,2]{0,1:T(2,128)(2,1)S(1)}, bf16[2048,2]{0,1:T(2,128)(2,1)}, u32[]{:S(2)}) copy-start(bf16[2048,2]{0,1:T(2,128)(2,1)} %param.22) | copy-start | bytes 24580
  40.9 4.4 %copy-start.15 = (f32[2]{0:T(128)S(1)}, f32[2]{0:T(128)}, u32[]{:S(2)}) copy-start(f32[2]{0:T(128)} %param.26) | copy-start | bytes 28
  41.7 4.3 %copy-start.5 = (f32[512,256]{1,0:T(8,128)}, f32[512,256]{1,0:T(8,128)S(1)}, u32[]{:S(2)}) copy-start(f32[512,256]{1,0:T(8,128)S(1)} %fusion.150) | copy-start | bytes 1572868
  41.7 4.8 %collective-permute-start = (f32[3,768]{1,0:T(4,128)S(1)}, f32[3,768]{1,0:T(4,128)S(1)}, u32[]{:S(2)}, u32[]{:S(2)}) collective-permute-start(f32[3,768]{1,0:T(4,128)S(1)} %pad_maximum_fusion.4), channel_id=1, source_target_pairs={{0,4},{4,8},{8,12},{12,16},{16,20},{20,24},{24,28},{1,5},{5,9},{9,... | collective-permute-start | bytes 27656 | tf_op jit(solution)/shard_map/ppermute | solution.py:16
  59.6 3.5 %copy-start.4 = (f32[512,256]{1,0:T(8,128)S(1)}, f32[512,256]{1,0:T(8,128)}, u32[]{:S(2)}) copy-start(f32[512,256]{1,0:T(8,128)} %copy-done.3) | copy-start | bytes 1572868
  59.6 3.5 %copy-start.6 = (f32[512,256]{1,0:T(8,128)S(1)}, f32[512,256]{1,0:T(8,128)}, u32[]{:S(2)}) copy-start(f32[512,256]{1,0:T(8,128)} %copy-done.5) | copy-start | bytes 1572868
  59.6 3.5 %copy-start.9 = (f32[1,1,256]{2,0,1:T(1,128)S(1)}, f32[1,1,256]{2,0,1:T(1,128)}, u32[]{:S(2)}) copy-start(f32[1,1,256]{2,0,1:T(1,128)} %get-tuple-element.113) | copy-start | bytes 3076
  59.6 3.5 %copy-start.10 = (f32[1,1,256]{2,0,1:T(1,128)S(1)}, f32[1,1,256]{2,0,1:T(1,128)}, u32[]{:S(2)}) copy-start(f32[1,1,256]{2,0,1:T(1,128)} %get-tuple-element.114) | copy-start | bytes 3076
  59.6 3.5 %copy-start.11 = (f32[1,1,256]{2,0,1:T(1,128)S(1)}, f32[1,1,256]{2,0,1:T(1,128)}, u32[]{:S(2)}) copy-start(f32[1,1,256]{2,0,1:T(1,128)} %get-tuple-element.115) | copy-start | bytes 3076
  59.6 3.5 %copy-start.12 = (f32[1,1,256]{2,0,1:T(1,128)S(1)}, f32[1,1,256]{2,0,1:T(1,128)}, u32[]{:S(2)}) copy-start(f32[1,1,256]{2,0,1:T(1,128)} %get-tuple-element.116) | copy-start | bytes 3076
  59.6 3.5 %copy-start.13 = (f32[1,1,256]{2,0,1:T(1,128)S(1)}, f32[1,1,256]{2,0,1:T(1,128)}, u32[]{:S(2)}) copy-start(f32[1,1,256]{2,0,1:T(1,128)} %get-tuple-element.117) | copy-start | bytes 3076
  59.6 3.5 %copy-start.14 = (f32[1,1,256]{2,0,1:T(1,128)S(1)}, f32[1,1,256]{2,0,1:T(1,128)}, u32[]{:S(2)}) copy-start(f32[1,1,256]{2,0,1:T(1,128)} %get-tuple-element.118) | copy-start | bytes 3076
  71.0 6.9 %copy-start.18 = (f32[128]{0:T(128)S(1)}, f32[128]{0:T(128)}, u32[]{:S(2)}) copy-start(f32[128]{0:T(128)} %param.28) | copy-start | bytes 1540
  77.8 95.8 %all-gather.7.cloned.1.call-start = ((), (), s32[]{:S(2)}) async-start(), calls=%async_computation.2 | async-start | bytes 1310720 | tf_op jit(solution)/shard_map/all_gather | solution.py:210
  139.5 6.6 %copy-start.2 = (bf16[512,2048]{1,0:T(8,128)(2,1)S(1)}, bf16[512,2048]{1,0:T(8,128)(2,1)}, u32[]{:S(2)}) copy-start(bf16[512,2048]{1,0:T(8,128)(2,1)} %all-gather.5.cloned.1.call-done) | copy-start | bytes 6291460
Sparse Core Ops, SparseCore 0:
  8.9 25.2 all-gather.4
  78.0 49.9 all-gather.8
  149.1 21.0 all-gather.6
where the time goes:
time: 184 us; the launch traced here: 183 us
  waiting for transfers between devices  59.6 us (32%)
  matrix products  49.9 us (27%)
  blocking collectives  22.6 us (12%)
  local copies, waits for them, and re-layouts  17.1 us (9%)
  other arithmetic  15.9 us (9%)
  between operations  13.9 us (8%)
  starting transfers between devices  3.64 us (2%)
    all_gather x1, waiting for transfers between devices, on_device(): every_map = lax.all_gather(stacked, 'seq', axis=0, tiled=True)  35 us
    all_gather x1, waiting for transfers between devices, on_device(): shard_piece = lax.all_gather(layer_in, 'head', axis=1, tiled=True)  23.5 us
    all_to_all x1, blocking collectives, on_device(): lax.all_to_all(out_weight, 'head', split_axis=1, concat_axis=0, tiled=True)  22.6 us
    dot_general x6, matrix products, on_device(): jnp.dot(shard_piece, weight, preferred_element_type=jnp.float32)  8.02 us
    dot_general x7, matrix products, compose(): jnp.einsum('...de,...ef->...df', later_map[0], earlier[1], precision=exac...  6.03 us
    dot_general x7, matrix products, unit_lower_inverse(): jnp.einsum('...rs,...st->...rt', inverse, middle, precision=exact_mode)  5.27 us
    dot_general x7, matrix products, unit_lower_inverse(): jnp.einsum('...rs,...st->...rt', linking, inverse, precision=exact_mode)  4.78 us
    dot_general x4, matrix products, advance(): jnp.einsum('hde,hef->hdf', block_maps[0], carry_state, precision=exact_mode)  4.67 us
  transfers between devices with their start and end apart: 4, of which 3 were waited for; matrix products, arithmetic and copies ran while one was open for 12% of the time, Pallas kernels for 0%

commit v1 on v0

v1 whole, which is shorter than its diff:
```python
import functools

import jax
import jax.numpy as jnp
from jax import lax
from jax.experimental import pallas as pl
from jax.experimental.pallas import tpu as pltpu
from jax.sharding import PartitionSpec as P

BLOCK = 128
PRIOR = 16
LANES = 128
GROUPS = 2
PER_GROUP = 2
MESH = pl.DeviceIdType.MESH
F32 = jnp.float32
BF16 = jnp.bfloat16
norm_floor = 0.0001


def bits_below(limit):
    found = []
    bit = limit // 2
    while bit:
        found.append(bit)
        bit //= 2
    return found


def low_bit(value):
    return value & -value


def meet(peers):
    barrier = pltpu.get_barrier_semaphore()
    expected = 0
    for present, device in peers:
        if present is True:
            pl.semaphore_signal(barrier, inc=1, device_id=device, device_id_type=MESH)
            expected = expected + 1
        else:

            @pl.when(present)
            def _():
                pl.semaphore_signal(barrier, inc=1, device_id=device, device_id_type=MESH)

            expected = expected + present.astype(jnp.int32)
    pl.semaphore_wait(barrier, expected)


def remote(source, target, send_sem, recv_sem, device):
    return pltpu.make_async_remote_copy(
        src_ref=source,
        dst_ref=target,
        send_sem=send_sem,
        recv_sem=recv_sem,
        device_id=device,
        device_id_type=MESH,
    )


def dot(left, right, contract=((1,), (0,))):
    return lax.dot_general(
        left.astype(BF16), right.astype(BF16), (contract, ((), ())), preferred_element_type=F32
    )


def split(value):
    high = value.astype(BF16)
    return high, (value - high.astype(F32)).astype(BF16)


def dot3(left, right, contract=((1,), (0,))):
    lh, ll = left if isinstance(left, tuple) else split(left)
    rh, rl = right if isinstance(right, tuple) else split(right)
    axis = contract[1][0]
    both = dot(jnp.concatenate([lh, lh], axis=1), jnp.concatenate([rh, rl], axis=axis), contract)
    return both + dot(ll, rh, contract)


def layer_kernel(
    seqs, n, heads,
    x_ref, wq, wk, wv, wg, beta_ref, step_ref, taps, rates, beta_bias, decay_bias, gain, w_ref,
    out_ref,
    w_all, w_flat, x_own, buf, prior, raw, local, reader, maps, slab,
    w_buf, pair_buf, go_buf, in_buf, hid,
    load_sem, x_sem, x_send, x_recv, p_send, p_recv, own_sem, w_send, w_recv,
    pair_sem, chain_send, chain_recv, h_send, h_recv,
):
    seq = lax.axis_index("seq")
    me = lax.axis_index("head")
    tokens, feats = x_ref.shape
    width = wq.shape[1]
    dim = LANES
    blocks = tokens // BLOCK
    columns = out_ref.shape[1]
    sends_each = GROUPS * PER_GROUP
    rows = tokens // sends_each
    group_rows = tokens // GROUPS
    group_blocks = blocks // GROUPS
    bits = bits_below(n)

    loads = [pltpu.make_async_copy(x_ref, x_own, x_sem)]
    for i, w in enumerate((wq, wk, wv, wg)):
        loads.append(
            pltpu.make_async_copy(w, w_all.at[:, pl.ds(i * width, width)], load_sem.at[i])
        )
    for load in loads:
        load.start()
    has_next = seq < seqs - 1
    has_before = seq > 0
    far_next = seq < seqs - 2
    far_before = seq >= 2
    odd = seq % 2
    is_odd = odd == 1
    mate = seq + 1 - 2 * odd
    peers = [(True, (seq, me ^ m)) for m in range(1, n)]
    peers += [(has_next, (seq + 1, me ^ m)) for m in range(n)]
    peers += [(has_before, (seq - 1, me ^ m)) for m in range(n)]
    peers += [(far_next, (seq + 2, me)), (far_before, (seq - 2, me))]
    meet(peers)

    def hop(m, bit, c):
        piece = pl.ds(c * rows, rows)
        source = x_ref.at[piece] if m == 0 else buf.at[m, piece]
        got = m | bit
        return remote(
            source, buf.at[got, piece], x_send.at[got, c], x_recv.at[got, c], (seq, me ^ bit)
        )

    hops = {}
    for bit in bits:
        for c in range(sends_each):
            hops[bit, c] = hop(0, bit, c)
            hops[bit, c].start()
    tails = [
        remote(
            x_ref.at[pl.ds(tokens - PRIOR, PRIOR)],
            prior.at[m],
            p_send.at[m],
            p_recv.at[m],
            (seq + 1, me ^ m),
        )
        for m in range(n)
    ]

    @pl.when(has_next)
    def _():
        for tail in tails:
            tail.start()

    w_flat[...] = jnp.zeros(w_flat.shape, F32)
    w_flat[pl.ds(0, heads), :] = beta_ref[...].astype(F32)
    w_flat[pl.ds(heads, heads), :] = step_ref[...].astype(F32)
    for i in range(w_flat.shape[1] // LANES):
        piece = pl.ds(i * LANES, LANES)
        w_all[piece, pl.ds(4 * width, LANES)] = w_flat[:, piece].T.astype(BF16)
    for load in loads:
        load.wait()

    def weights_of(m):
        start = pl.multiple_of((me ^ m) * feats, LANES)
        return w_all[pl.ds(start, feats), :]

    def arrive(m, c):
        hops[m, c].wait_recv()
        for bit in bits:
            if bit < low_bit(m):
                hops[m | bit, c] = hop(m, bit, c)
                hops[m | bit, c].start()

    def add(m, g):
        piece = pl.ds(g * group_rows, group_rows)
        here = pl.ds(PRIOR + g * group_rows, group_rows)
        values = x_own[piece, :] if m == 0 else buf[m, piece, :]
        term = jnp.dot(values, weights_of(m), preferred_element_type=F32)
        if m == 0:
            raw[here, :] = term
        else:
            raw[here, :] = raw[here, :] + term

    for g in range(GROUPS):
        add(0, g)
    for g in range(GROUPS):
        for c in range(g * PER_GROUP, (g + 1) * PER_GROUP):
            arrive(1, c)
        add(1, g)

    @pl.when(has_before)
    def _():
        total = jnp.zeros((PRIOR, raw.shape[1]), F32)
        for m in range(n):
            tails[m].wait_recv()
            total = total + jnp.dot(prior[m], weights_of(m), preferred_element_type=F32)
        raw[pl.ds(0, PRIOR), :] = total

    @pl.when(jnp.logical_not(has_before))
    def _():
        raw[pl.ds(0, PRIOR), :] = jnp.zeros((PRIOR, raw.shape[1]), F32)

    row = lax.broadcasted_iota(jnp.int32, (BLOCK, BLOCK), 0)
    col = lax.broadcasted_iota(jnp.int32, (BLOCK, BLOCK), 1)
    within = row >= col
    before = row > col
    eye = (row == col).astype(F32)
    lower = within.astype(F32)
    lane = lax.broadcasted_iota(jnp.int32, (1, LANES), 1)
    offset = jnp.zeros((1, LANES), F32)
    rate = jnp.zeros((1, LANES), F32)
    for h in range(heads):
        offset = jnp.where(lane == h, beta_bias[h], offset)
        offset = jnp.where(lane == heads + h, decay_bias[h], offset)
        rate = jnp.where(lane == heads + h, rates[h], rate)
    rate = -jnp.exp(rate)

    def mixed(kind, h, b):
        base = kind * width + h * dim
        start = PRIOR + b * BLOCK
        total = None
        for s in range(taps.shape[1]):
            tap = taps[kind, pl.ds(s, 1), pl.ds(h * dim, dim)]
            term = tap * raw[pl.ds(start - s, BLOCK), pl.ds(base, dim)]
            total = term if total is None else total + term
        return total * jax.nn.sigmoid(total)

    def unit(values):
        return values * lax.rsqrt(jnp.sum(values * values, axis=-1, keepdims=True) + 1.0)

    def block_terms(g, midway):
        pairs = [(b, h) for b in range(g * group_blocks, (g + 1) * group_blocks)
                 for h in range(heads)]
        betas, runs, acrosses = {}, {}, {}
        for b in range(g * group_blocks, (g + 1) * group_blocks):
            small = raw[pl.ds(PRIOR + b * BLOCK, BLOCK), pl.ds(4 * width, LANES)] + offset
            betas[b] = jax.nn.sigmoid(small)
            steps = rate * (jnp.maximum(small, 0.0) + jnp.log1p(jnp.exp(-jnp.abs(small))))
            runs[b] = jnp.dot(
                lower, steps, precision=lax.Precision.HIGHEST, preferred_element_type=F32
            )
            acrosses[b] = runs[b].T
        lows, mixes, sides, weighteds, reads, ends = [], [], [], [], [], []
        for b, h in pairs:
            q = unit(mixed(0, h, b))
            k = unit(mixed(1, h, b))
            v = mixed(2, h, b)
            beta = betas[b][:, h : h + 1]
            down = runs[b][:, heads + h : heads + h + 1]
            along = acrosses[b][heads + h : heads + h + 1, :]
            last = down[BLOCK - 1 : BLOCK, :]
            decay = jnp.where(within, jnp.exp(jnp.minimum(down - along, 0.0)), 0.0)
            grams = dot3(jnp.concatenate([q, k], axis=0), k, ((1,), (1,)))
            mixes.append(decay * grams[:BLOCK])
            lows.append(jnp.where(before, beta * decay * grams[BLOCK:], 0.0))
            growth = jnp.exp(down)
            sides.append(jnp.concatenate([beta * v, (beta * growth) * k], axis=1))
            weighteds.append((jnp.exp(last - down) * k).T)
            reads.append(growth * q)
            ends.append(jnp.exp(last))
        inverses = [eye - jnp.where((row // 2 == col // 2), low, 0.0) for low in lows]
        span = 2
        while span < BLOCK:
            linked = (row // (2 * span) == col // (2 * span)) & (row // span > col // span)
            shares = [split(inv) for inv in inverses]
            middles = [
                dot3(jnp.where(linked, low, 0.0), share) for low, share in zip(lows, shares)
            ]
            inverses = [
                inv - dot3(share, middle)
                for inv, share, middle in zip(inverses, shares, middles)
            ]
            span *= 2
        midway()
        solved = [split(dot3(inv, side)) for inv, side in zip(inverses, sides)]
        found = {}
        for i, (b, h) in enumerate(pairs):
            got = dot3(weighteds[i], solved[i])
            transit = ends[i] * eye - got[:, dim:]
            reader[h, b, pl.ds(BLOCK, dim), :] = transit.astype(BF16)
            maps[h, b] = got[:, :dim]
            found[b, h] = (transit, got[:, :dim])

        def outputs():
            for i, (b, h) in enumerate(pairs):
                got = dot3(mixes[i], solved[i])
                local[h, pl.ds(b * BLOCK, BLOCK), :] = got[:, :dim]
                reader[h, b, pl.ds(0, BLOCK), :] = (reads[i] - got[:, dim:]).astype(BF16)

        return found, outputs

    far = sorted(range(2, n), key=lambda m: (-low_bit(m), m))
    joined = [None] * heads
    for g in range(GROUPS):
        mine = range(g * PER_GROUP, (g + 1) * PER_GROUP)
        for m in far:
            for c in mine:
                if (m, "in", c) not in hops:
                    arrive(m, c)
            add(m, g)

        def midway():
            if g + 1 < GROUPS:
                for m in far:
                    if low_bit(m) > 1:
                        c = (g + 1) * PER_GROUP
                        arrive(m, c)
                        hops[m, "in", c] = None

        found, outputs = block_terms(g, midway)
        for h in range(heads):
            for b in range(g * group_blocks, (g + 1) * group_blocks):
                transit, carried = found[b, h]
                if joined[h] is None:
                    joined[h] = jnp.concatenate([transit, carried], axis=1)
                else:
                    moved = dot3(transit, joined[h])
                    joined[h] = jnp.concatenate(
                        [moved[:, :dim], moved[:, dim:] + carried], axis=1
                    )
        if g + 1 < GROUPS:
            outputs()
        else:
            for h in range(heads):
                slab[h] = joined[h].astype(slab.dtype)

    swaps = [
        remote(slab.at[h], pair_buf.at[h], pair_sem.at[0, h], pair_sem.at[1, h], (mate, me))
        for h in range(heads)
    ]
    for swap in swaps:
        swap.start()

    def columns_of(m):
        return pl.ds(pl.multiple_of((me ^ m) * columns, LANES), columns)

    own = pltpu.make_async_copy(w_ref.at[:, columns_of(0)], w_buf.at[0], own_sem)
    own.start()
    moves = []
    for m in range(1, n):
        move = remote(
            w_ref.at[:, columns_of(m)], w_buf.at[m], w_send.at[m], w_recv.at[m], (seq, me ^ m)
        )
        move.start()
        moves.append(move)
    outputs()

    firsts, comps = [], []
    for h in range(heads):
        swaps[h].wait()
        here = slab[h].astype(F32)
        there = pair_buf[h].astype(F32)
        first = jnp.where(is_odd, there, here)
        second = jnp.where(is_odd, here, there)
        moved = dot(second[:, :dim], first)
        comps.append((moved[:, :dim], moved[:, dim:] + second[:, dim:]))
        firsts.append(first)
    sends = [
        remote(go_buf.at[h], in_buf.at[h], chain_send.at[h], chain_recv.at[h], (seq + 2, me))
        for h in range(heads)
    ]

    @pl.when(jnp.logical_not(far_before))
    def _():
        in_buf[...] = jnp.zeros(in_buf.shape, in_buf.dtype)

    for h in range(heads):

        @pl.when(far_before)
        def _():
            sends[h].wait_recv()

        @pl.when(far_next)
        def _():
            go_buf[h] = (dot(comps[h][0], in_buf[h]) + comps[h][1]).astype(go_buf.dtype)
            sends[h].start()

    states = []
    for h in range(heads):
        arrived = in_buf[h].astype(F32)
        later = dot(firsts[h][:, :dim], arrived) + firsts[h][:, dim:]
        states.append(jnp.where(is_odd, later, arrived))

    lifts = {}

    def lift(m, bit, b):
        got = m | bit
        return remote(
            hid.at[m, b], hid.at[got, b], h_send.at[got, b], h_recv.at[got, b], (seq, me ^ bit)
        )

    def forward(m, b):
        limit = n if m == 0 else low_bit(m)
        for bit in bits:
            if bit < limit:
                lifts[m | bit, b] = lift(m, bit, b)
                lifts[m | bit, b].start()

    for b in range(blocks):
        for h in range(heads):
            got = dot(reader[h, b], states[h])
            states[h] = got[BLOCK:] + maps[h, b]
            head_out = got[:BLOCK] + local[h, pl.ds(b * BLOCK, BLOCK), :]
            gate = raw[pl.ds(PRIOR + b * BLOCK, BLOCK), pl.ds(3 * width + h * dim, dim)]
            scaled = head_out * lax.rsqrt(
                jnp.mean(head_out * head_out, axis=-1, keepdims=True) + norm_floor
            )
            hid[0, b, :, pl.ds(h * dim, dim)] = (
                scaled * gain[...] * (gate * jax.nn.sigmoid(gate))
            ).astype(BF16)
        forward(0, b)

    own.wait()
    for move in moves:
        move.wait()
    order = sorted(range(1, n), key=lambda m: (m != 1, -low_bit(m), m))
    for b in range(blocks):
        total = jnp.dot(hid[0, b], w_buf[0], preferred_element_type=F32)
        for m in order:
            lifts[m, b].wait_recv()
            forward(m, b)
            total = total + jnp.dot(hid[m, b], w_buf[m], preferred_element_type=F32)
        out_ref[pl.ds(b * BLOCK, BLOCK), :] = total.astype(BF16)

    for key, copy in hops.items():
        if copy is not None:
            copy.wait_send()
    for copy in lifts.values():
        copy.wait_send()

    @pl.when(has_next)
    def _():
        for tail in tails:
            tail.wait_send()

    @pl.when(far_next)
    def _():
        for send in sends:
            send.wait_send()


def on_device(
    seqs, n,
    layer_in, query_weight, key_weight, value_weight, gate_weight, beta_weight, decay_weight,
    conv_weight, decay_log, beta_bias, decay_bias, norm_gain, out_weight,
):
    tokens, feats = layer_in.shape
    model, width = query_weight.shape
    heads = beta_weight.shape[1]
    dim = width // heads
    blocks = tokens // BLOCK
    total_width = 4 * width + LANES
    columns = out_weight.shape[1] // n
    vmem = pl.BlockSpec(memory_space=pltpu.VMEM)
    smem = pl.BlockSpec(memory_space=pltpu.SMEM)
    anywhere = pl.BlockSpec(memory_space=pl.ANY)
    dma = pltpu.SemaphoreType.DMA
    sends_each = GROUPS * PER_GROUP
    wire = BF16 if seqs <= 8 else F32
    return pl.pallas_call(
        functools.partial(layer_kernel, seqs, n, heads),
        out_shape=jax.ShapeDtypeStruct((tokens, columns), BF16),
        in_specs=[anywhere] * 5 + [vmem] * 3 + [smem] * 3 + [vmem, anywhere],
        out_specs=vmem,
        scratch_shapes=[
            pltpu.VMEM((model, total_width), BF16),
            pltpu.VMEM((LANES, model), F32),
            pltpu.VMEM((tokens, feats), BF16),
            pltpu.VMEM((n, tokens, feats), BF16),
            pltpu.VMEM((n, PRIOR, feats), BF16),
            pltpu.VMEM((PRIOR + tokens, total_width), F32),
            pltpu.VMEM((heads, tokens, dim), F32),
            pltpu.VMEM((heads, blocks, BLOCK + dim, dim), BF16),
            pltpu.VMEM((heads, blocks, dim, dim), F32),
            pltpu.VMEM((heads, dim, 2 * dim), wire),
            pltpu.VMEM((n, width, columns), BF16),
            pltpu.VMEM((heads, dim, 2 * dim), wire),
            pltpu.VMEM((heads, dim, dim), wire),
            pltpu.VMEM((heads, dim, dim), wire),
            pltpu.VMEM((n, blocks, BLOCK, width), BF16),
            dma((4,)),
            dma(()),
            dma((n, sends_each)),
            dma((n, sends_each)),
            dma((n,)),
            dma((n,)),
            dma(()),
            dma((n,)),
            dma((n,)),
            dma((2, heads)),
            dma((heads,)),
            dma((heads,)),
            dma((n, blocks)),
            dma((n, blocks)),
        ],
        compiler_params=pltpu.CompilerParams(
            collective_id=0, has_side_effects=True, vmem_limit_bytes=60 * 1024 * 1024
        ),
    )(
        layer_in, query_weight, key_weight, value_weight, gate_weight,
        beta_weight.T, decay_weight.T, conv_weight.transpose(1, 0, 2),
        decay_log, beta_bias, decay_bias, norm_gain[None], out_weight,
    )


def solution(mesh):
    return jax.shard_map(
        functools.partial(on_device, mesh.shape["seq"], mesh.shape["head"]),
        mesh=mesh,
        in_specs=(
            P("seq", "head"),
            P(None, "head"),
            P(None, "head"),
            P(None, "head"),
            P(None, "head"),
            P(None, "head"),
            P(None, "head"),
            P(None, None, "head"),
            P("head"),
            P("head"),
            P("head"),
            P(),
            P("head", None),
        ),
        out_specs=P("seq", "head"),
        check_vma=False,
    )
```

time: 184 us -> 54.5 us (0.30)
  the two profiles are of different devices: /device:TPU:0 before, /device:TPU:25 now
where the time goes in v1:
time: 54.5 us; the launch traced here: 54.3 us
  Pallas kernels  52.5 us (96%)
  local copies, waits for them, and re-layouts  1.87 us (3%)
    pallas_call x1, Pallas kernels, on_device(): pl.pallas_call(functools.partial(layer_kernel, seqs, n, heads), out_shape...  52.5 us
    unnamed x1, local copies, waits for them, and re-layouts  1.87 us

profile of v1, /device:TPU:25, one launch (start us, length us, event | category | flops | bytes accessed | tf_op | source)
XLA Modules:
  0.0 54.3 jit_solution(11926730993428501365)
XLA Ops:
  0.0 52.5 %shard_map.127 = bf16[512,512]{1,0:T(8,128)(2,1)} custom-call(bf16[512,512]{1,0:T(8,128)(2,1)} %x_ref.1, bf16[2048,256]{1,0:T(8,128)(2,1)} %wq.1, bf16[2048,256]{1,0:T(8,128)(2,1)} %wk.1, bf16[2048,256]{1,0:T(8,128)(2,1)} %wv.1, bf16[2048,256]{1,0:T(8,128)(2,1)} %wg.1, bf16[2,2048]{1,0:T(2,128)(2,1)} %bitcast.5, bf16[2,2048]{1,0:T(2,128)(2,1)} %bitcast.6, ...), custom_call_target="tpu_custom_call" | custom-call | tf_op jit(solution)/shard_map/pallas_call | solution.py:458
  52.5 1.9 %copy.15 = bf16[512,512]{1,0:T(8,128)(2,1)} copy(bf16[512,512]{1,0:T(8,128)(2,1)} %shard_map.127) | data formatting | bytes 1048576

commit v2 on v1

--- a/solution.py
+++ b/solution.py
@@ -80,11 +80,12 @@
 
 def layer_kernel(
     seqs, n, heads,
-    x_ref, wq, wk, wv, wg, beta_ref, step_ref, taps, rates, beta_bias, decay_bias, gain, w_ref,
+    x_ref, wq, wk, wv, wg, beta_in, step_in, taps_in, rates_in, bias_in, shift_in, gain_in, w_ref,
     out_ref,
     w_all, w_flat, x_own, buf, prior, raw, local, reader, maps, slab,
     w_buf, pair_buf, go_buf, in_buf, hid,
-    load_sem, x_sem, x_send, x_recv, p_send, p_recv, own_sem, w_send, w_recv,
+    beta_ref, step_ref, taps, gain, rates, beta_bias, decay_bias,
+    load_sem, small_sem, x_sem, x_send, x_recv, p_send, p_recv, own_sem, w_send, w_recv,
     pair_sem, chain_send, chain_recv, h_send, h_recv,
 ):
     seq = lax.axis_index("seq")
@@ -105,7 +106,14 @@
         loads.append(
             pltpu.make_async_copy(w, w_all.at[:, pl.ds(i * width, width)], load_sem.at[i])
         )
-    for load in loads:
+    smalls = [
+        pltpu.make_async_copy(source, target, small_sem.at[i])
+        for i, (source, target) in enumerate((
+            (beta_in, beta_ref), (step_in, step_ref), (taps_in, taps), (gain_in, gain),
+            (rates_in, rates), (bias_in, beta_bias), (shift_in, decay_bias),
+        ))
+    ]
+    for load in loads + smalls:
         load.start()
     has_next = seq < seqs - 1
     has_before = seq > 0
@@ -128,11 +136,6 @@
             source, buf.at[got, piece], x_send.at[got, c], x_recv.at[got, c], (seq, me ^ bit)
         )
 
-    hops = {}
-    for bit in bits:
-        for c in range(sends_each):
-            hops[bit, c] = hop(0, bit, c)
-            hops[bit, c].start()
     tails = [
         remote(
             x_ref.at[pl.ds(tokens - PRIOR, PRIOR)],
@@ -149,6 +152,13 @@
         for tail in tails:
             tail.start()
 
+    hops = {}
+    for bit in bits:
+        for c in range(sends_each):
+            hops[bit, c] = hop(0, bit, c)
+            hops[bit, c].start()
+    for load in smalls:
+        load.wait()
     w_flat[...] = jnp.zeros(w_flat.shape, F32)
     w_flat[pl.ds(0, heads), :] = beta_ref[...].astype(F32)
     w_flat[pl.ds(heads, heads), :] = step_ref[...].astype(F32)
@@ -186,17 +196,18 @@
             arrive(1, c)
         add(1, g)
 
-    @pl.when(has_before)
-    def _():
-        total = jnp.zeros((PRIOR, raw.shape[1]), F32)
-        for m in range(n):
-            tails[m].wait_recv()
-            total = total + jnp.dot(prior[m], weights_of(m), preferred_element_type=F32)
-        raw[pl.ds(0, PRIOR), :] = total
-
-    @pl.when(jnp.logical_not(has_before))
-    def _():
-        raw[pl.ds(0, PRIOR), :] = jnp.zeros((PRIOR, raw.shape[1]), F32)
+    def add_prior():
+        @pl.when(has_before)
+        def _():
+            total = jnp.zeros((PRIOR, raw.shape[1]), F32)
+            for m in range(n):
+                tails[m].wait_recv()
+                total = total + jnp.dot(prior[m], weights_of(m), preferred_element_type=F32)
+            raw[pl.ds(0, PRIOR), :] = total
+
+        @pl.when(jnp.logical_not(has_before))
+        def _():
+            raw[pl.ds(0, PRIOR), :] = jnp.zeros((PRIOR, raw.shape[1]), F32)
 
     row = lax.broadcasted_iota(jnp.int32, (BLOCK, BLOCK), 0)
     col = lax.broadcasted_iota(jnp.int32, (BLOCK, BLOCK), 1)
@@ -287,6 +298,16 @@
 
         return found, outputs
 
+    def columns_of(m):
+        return pl.ds(pl.multiple_of((me ^ m) * columns, LANES), columns)
+
+    own = pltpu.make_async_copy(w_ref.at[:, columns_of(0)], w_buf.at[0], own_sem)
+    moves = {
+        m: remote(
+            w_ref.at[:, columns_of(m)], w_buf.at[m], w_send.at[m], w_recv.at[m], (seq, me ^ m)
+        )
+        for m in range(1, n)
+    }
     far = sorted(range(2, n), key=lambda m: (-low_bit(m), m))
     joined = [None] * heads
     for g in range(GROUPS):
@@ -296,8 +317,14 @@
                 if (m, "in", c) not in hops:
                     arrive(m, c)
             add(m, g)
+        if g == 0:
+            add_prior()
 
         def midway():
+            if g == 0:
+                own.start()
+                for m in far:
+                    moves[m].start()
             if g + 1 < GROUPS:
                 for m in far:
                     if low_bit(m) > 1:
@@ -328,19 +355,8 @@
     ]
     for swap in swaps:
         swap.start()
-
-    def columns_of(m):
-        return pl.ds(pl.multiple_of((me ^ m) * columns, LANES), columns)
-
-    own = pltpu.make_async_copy(w_ref.at[:, columns_of(0)], w_buf.at[0], own_sem)
-    own.start()
-    moves = []
-    for m in range(1, n):
-        move = remote(
-            w_ref.at[:, columns_of(m)], w_buf.at[m], w_send.at[m], w_recv.at[m], (seq, me ^ m)
-        )
-        move.start()
-        moves.append(move)
+    moves[1].start()
+
     outputs()
 
     firsts, comps = [], []
@@ -409,7 +425,7 @@
         forward(0, b)
 
     own.wait()
-    for move in moves:
+    for move in moves.values():
         move.wait()
     order = sorted(range(1, n), key=lambda m: (m != 1, -low_bit(m), m))
     for b in range(blocks):
@@ -450,7 +466,6 @@
     total_width = 4 * width + LANES
     columns = out_weight.shape[1] // n
     vmem = pl.BlockSpec(memory_space=pltpu.VMEM)
-    smem = pl.BlockSpec(memory_space=pltpu.SMEM)
     anywhere = pl.BlockSpec(memory_space=pl.ANY)
     dma = pltpu.SemaphoreType.DMA
     sends_each = GROUPS * PER_GROUP
@@ -458,7 +473,7 @@
     return pl.pallas_call(
         functools.partial(layer_kernel, seqs, n, heads),
         out_shape=jax.ShapeDtypeStruct((tokens, columns), BF16),
-        in_specs=[anywhere] * 5 + [vmem] * 3 + [smem] * 3 + [vmem, anywhere],
+        in_specs=[anywhere] * 13,
         out_specs=vmem,
         scratch_shapes=[
             pltpu.VMEM((model, total_width), BF16),
@@ -476,7 +491,15 @@
             pltpu.VMEM((heads, dim, dim), wire),
             pltpu.VMEM((heads, dim, dim), wire),
             pltpu.VMEM((n, blocks, BLOCK, width), BF16),
+            pltpu.VMEM((heads, model), BF16),
+            pltpu.VMEM((heads, model), BF16),
+            pltpu.VMEM((conv_weight.shape[1], conv_weight.shape[0], width), F32),
+            pltpu.VMEM((1, dim), F32),
+            pltpu.SMEM((heads,), F32),
+            pltpu.SMEM((heads,), F32),
+            pltpu.SMEM((heads,), F32),
             dma((4,)),
+            dma((7,)),
             dma(()),
             dma((n, sends_each)),
             dma((n, sends_each)),

time: 54.5 us -> 48.5 us (0.89)
  Pallas kernels: 52.5 us -> 46.5 us
    pallas_call x1, Pallas kernels: 52.5 us -> 46.5 us  [on_device(): pl.pallas_call(functools.partial(layer_kernel, seqs, n, heads), out_shape...]
where the time goes in v2:
time: 48.5 us; the launch traced here: 48.4 us
  Pallas kernels  46.5 us (96%)
  local copies, waits for them, and re-layouts  1.87 us (4%)
    pallas_call x1, Pallas kernels, on_device(): pl.pallas_call(functools.partial(layer_kernel, seqs, n, heads), out_shape...  46.5 us
    unnamed x1, local copies, waits for them, and re-layouts  1.87 us

profile of v2, /device:TPU:25, one launch (start us, length us, event | category | flops | bytes accessed | tf_op | source)
XLA Modules:
  0.0 48.4 jit_solution(11237155240878475287)
XLA Ops:
  0.0 46.5 %shard_map.127 = bf16[512,512]{1,0:T(8,128)(2,1)} custom-call(bf16[512,512]{1,0:T(8,128)(2,1)} %x_ref.1, bf16[2048,256]{1,0:T(8,128)(2,1)} %wq.1, bf16[2048,256]{1,0:T(8,128)(2,1)} %wk.1, bf16[2048,256]{1,0:T(8,128)(2,1)} %wv.1, bf16[2048,256]{1,0:T(8,128)(2,1)} %wg.1, bf16[2,2048]{1,0:T(2,128)(2,1)} %bitcast.5, bf16[2,2048]{1,0:T(2,128)(2,1)} %bitcast.6, ...), custom_call_target="tpu_custom_call" | custom-call | tf_op jit(solution)/shard_map/pallas_call | solution.py:473
  46.5 1.9 %copy.15 = bf16[512,512]{1,0:T(8,128)(2,1)} copy(bf16[512,512]{1,0:T(8,128)(2,1)} %shard_map.127) | data formatting | bytes 1048576

commit v3 on v2

--- a/solution.py
+++ b/solution.py
@@ -358,6 +358,10 @@
     moves[1].start()
 
     outputs()
+    for h in range(heads):
+        place = pl.ds(PRIOR, tokens), pl.ds(3 * width + h * dim, dim)
+        gate = raw[place]
+        raw[place] = gain[...] * (gate * jax.nn.sigmoid(gate))
 
     firsts, comps = [], []
     for h in range(heads):
@@ -420,7 +424,7 @@
                 jnp.mean(head_out * head_out, axis=-1, keepdims=True) + norm_floor
             )
             hid[0, b, :, pl.ds(h * dim, dim)] = (
-                scaled * gain[...] * (gate * jax.nn.sigmoid(gate))
+                scaled * gate
             ).astype(BF16)
         forward(0, b)
 
@@ -472,7 +476,7 @@
     wire = BF16 if seqs <= 8 else F32
     return pl.pallas_call(
         functools.partial(layer_kernel, seqs, n, heads),
-        out_shape=jax.ShapeDtypeStruct((tokens, columns), BF16),
+        out_shape=pltpu.VMEM((tokens, columns), BF16),
         in_specs=[anywhere] * 13,
         out_specs=vmem,
         scratch_shapes=[

time: 48.5 us -> 46.7 us (0.963)
  local copies, waits for them, and re-layouts: 1.87 us -> 0.8 us
  Pallas kernels: 46.5 us -> 45.7 us
    unnamed x1, local copies, waits for them, and re-layouts: 1.87 us -> 0.8 us
    pallas_call x1, Pallas kernels: 46.5 us -> 45.7 us  [on_device(): pl.pallas_call(functools.partial(layer_kernel, seqs, n, heads), out_shape...]
where the time goes in v3:
time: 46.7 us; the launch traced here: 46.5 us
  Pallas kernels  45.7 us (98%)
  local copies, waits for them, and re-layouts  0.8 us (2%)
    pallas_call x1, Pallas kernels, on_device(): pl.pallas_call(functools.partial(layer_kernel, seqs, n, heads), out_shape...  45.7 us

profile of v3, /device:TPU:25, one launch (start us, length us, event | category | flops | bytes accessed | tf_op | source)
XLA Modules:
  0.0 46.5 jit_solution(10341289737267177906)
XLA Ops:
  0.0 45.7 %shard_map.127 = bf16[512,512]{1,0:T(8,128)(2,1)S(1)} custom-call(bf16[512,512]{1,0:T(8,128)(2,1)} %x_ref.1, bf16[2048,256]{1,0:T(8,128)(2,1)} %wq.1, bf16[2048,256]{1,0:T(8,128)(2,1)} %wk.1, bf16[2048,256]{1,0:T(8,128)(2,1)} %wv.1, bf16[2048,256]{1,0:T(8,128)(2,1)} %wg.1, bf16[2,2048]{1,0:T(2,128)(2,1)} %bitcast.5, bf16[2,2048]{1,0:T(2,128)(2,1)} %bitcast.6, ...), custom_call_target="tpu_custom_call" | custom-call | tf_op jit(solution)/shard_map/pallas_call | solution.py:477
  45.7 0.8 %copy.15 = bf16[512,512]{1,0:T(8,128)(2,1)} copy(bf16[512,512]{1,0:T(8,128)(2,1)S(1)} %shard_map.127) | data formatting | bytes 1048576
